TPU v7x, 32 devices: a whole 2x2x4 slice. The times are simulated.
32 devices in a mesh: dp: 4 (over x, y), tp: 8 (over z, core).
Axes of the slice: x: 2, y: 2, z: 4, core: 2. Of those that a mesh axis runs over, the one named last changes fastest.
Arguments:
- hidden: bfloat16 [4, 4096, 1536], P('dp'), parts along dimension 0
- norm_w: bfloat16 [2, 1536], replicated
- w_z: bfloat16 [2, 1536, 3072], P(None, None, 'tp')
- w_x: bfloat16 [2, 1536, 3072], P(None, None, 'tp')
- w_bc: bfloat16 [2, 1536, 256], replicated
- w_dt: bfloat16 [2, 1536, 48], P(None, None, 'tp')
- conv_x: bfloat16 [2, 4, 3072], P(None, None, 'tp')
- conv_bc: bfloat16 [2, 4, 256], replicated
- bias_x: bfloat16 [2, 3072], P(None, 'tp')
- bias_bc: bfloat16 [2, 256], replicated
- dt_bias: float32 [2, 48], P(None, 'tp')
- a_log: float32 [2, 48], P(None, 'tp')
- d_skip: float32 [2, 48], P(None, 'tp')
- gate_w: bfloat16 [2, 3072], P(None, 'tp')
- w_out: bfloat16 [2, 3072, 1536], P(None, 'tp')
Outputs:
- output: bfloat16 [4, 4096, 1536], P('dp'), parts along dimension 0
There are 4 independent parts. A program takes and returns all parts, laid end to end along the dimension named above; an argument that names none is the same for every part.
All inputs are finite; a program needn't handle non-finite values.
Results may differ from a plain program's by a relative error of at most 0.0138432.
Values sent between devices are 32-bit elements.
A program may use at most 1 GiB of HBM per device.

v0:
```python
import jax
import jax.numpy as jnp
from jax import lax
from jax.sharding import PartitionSpec as P

EPSILON = 1e-5
CONV_WIDTH = 4
BLOCK_LEN = 256
FULL_PRECISION = lax.Precision.HIGHEST


def causal_conv(seq_in, kernel, conv_bias):
    n_steps = seq_in.shape[1]
    padded = jnp.pad(seq_in, ((0, 0), (CONV_WIDTH - 1, 0), (0, 0)))
    conv_sum = conv_bias.astype(jnp.float32)
    for tap_index in range(CONV_WIDTH):
        conv_sum = conv_sum + padded[:, tap_index:tap_index + n_steps, :].astype(jnp.float32) * kernel[tap_index].astype(jnp.float32)
    return conv_sum


def ssd_blocks(x_heads, dt_val, a_vals, b_in, c_in):
    n_batch, n_steps, n_heads, head_width = x_heads.shape
    n_state = b_in.shape[-1]
    n_blocks = n_steps // BLOCK_LEN
    x_blocks = x_heads.reshape(n_batch, n_blocks, BLOCK_LEN, n_heads, head_width)
    dt_blocks = dt_val.reshape(n_batch, n_blocks, BLOCK_LEN, n_heads)
    b_blocks = b_in.reshape(n_batch, n_blocks, BLOCK_LEN, n_state)
    c_blocks = c_in.reshape(n_batch, n_blocks, BLOCK_LEN, n_state)
    a_cum = jnp.cumsum(a_vals.reshape(n_batch, n_blocks, BLOCK_LEN, n_heads), axis=2)
    a_cum_t = jnp.swapaxes(a_cum, 2, 3)
    seg_sum = a_cum_t[..., :, None] - a_cum_t[..., None, :]
    step_ids = jnp.arange(BLOCK_LEN)
    lower_tri = step_ids[:, None] >= step_ids[None, :]
    c_dot_b = jnp.einsum('bcin,bcjn->bcij', c_blocks, b_blocks, precision=FULL_PRECISION)
    mix_mat = jnp.where(lower_tri, jnp.exp(jnp.minimum(seg_sum, 0.0)), 0.0) * c_dot_b[:, :, None]
    x_dt = x_blocks * dt_blocks[..., None]
    y_in = jnp.einsum('bchij,bcjhp->bcihp', mix_mat, x_dt, precision=FULL_PRECISION)
    a_last = a_cum[:, :, -1, :]
    tail_decay = jnp.exp(a_last[:, :, None, :] - a_cum)
    block_states = jnp.einsum('bcjn,bcjhp->bchpn', b_blocks, x_dt * tail_decay[..., None], precision=FULL_PRECISION)
    block_ends = jnp.swapaxes(jnp.cumsum(a_last, axis=1), 1, 2)
    block_starts = block_ends - jnp.swapaxes(a_last, 1, 2)
    block_ids = jnp.arange(n_blocks)
    earlier = block_ids[:, None] > block_ids[None, :]
    carry_mat = jnp.where(earlier, jnp.exp(jnp.minimum(block_starts[..., :, None] - block_ends[..., None, :], 0.0)), 0.0)
    s_in = jnp.einsum('bhck,bkhpn->bchpn', carry_mat, block_states, precision=FULL_PRECISION)
    y_st = jnp.einsum('bcin,bchpn->bcihp', c_blocks, s_in, precision=FULL_PRECISION) * jnp.exp(a_cum)[..., None]
    return (y_in + y_st).reshape(n_batch, n_steps, n_heads, head_width)


def mixer_layer(current, norm_w, w_z, w_x, w_bc, w_dt, conv_x, conv_bc, bias_x, bias_bc, dt_bias, a_log, d_skip, gate_w, w_out, inner_width):
    n_batch = current.shape[0]
    n_steps = current.shape[1]
    n_heads = dt_bias.shape[0]
    local_width = w_x.shape[-1]
    state_dim = w_bc.shape[-1] // 2
    residual = current.astype(jnp.float32)
    normed = (residual * lax.rsqrt(jnp.mean(residual * residual, axis=-1, keepdims=True) + EPSILON) * norm_w.astype(jnp.float32)).astype(jnp.bfloat16)
    gate_z = jnp.einsum('btd,de->bte', normed, w_z, preferred_element_type=jnp.float32).astype(jnp.bfloat16)
    x_pre = jnp.einsum('btd,de->bte', normed, w_x, preferred_element_type=jnp.float32).astype(jnp.bfloat16)
    bc_pre = jnp.einsum('btd,de->bte', normed, w_bc, preferred_element_type=jnp.float32).astype(jnp.bfloat16)
    dt_pre = jnp.einsum('btd,de->bte', normed, w_dt, preferred_element_type=jnp.float32).astype(jnp.bfloat16)
    x_act = jax.nn.silu(causal_conv(x_pre, conv_x, bias_x))
    bc_act = jax.nn.silu(causal_conv(bc_pre, conv_bc, bias_bc))
    dt_val = jax.nn.softplus(dt_pre.astype(jnp.float32) + dt_bias)
    a_vals = -dt_val * jnp.exp(a_log)
    x_heads = x_act.reshape(n_batch, n_steps, n_heads, local_width // n_heads)
    y_heads = ssd_blocks(x_heads, dt_val, a_vals, bc_act[..., :state_dim], bc_act[..., state_dim:]) + d_skip[:, None] * x_heads
    gated_v = y_heads.reshape(n_batch, n_steps, local_width) * jax.nn.silu(gate_z.astype(jnp.float32))
    part_sq = jnp.sum(gated_v * gated_v, axis=-1, keepdims=True)
    total_sq = lax.psum(part_sq, 'tp')
    normed_y = (gated_v * lax.rsqrt(total_sq / inner_width + EPSILON) * gate_w.astype(jnp.float32)).astype(jnp.bfloat16)
    part_out = jnp.einsum('bte,ed->btd', normed_y, w_out, preferred_element_type=jnp.float32)
    full_out = lax.psum(part_out, 'tp')
    return (residual + full_out).astype(jnp.bfloat16)


def solution(mesh):
    tp_size = mesh.shape['tp']
    rep_spec = P()
    col_spec = P(None, None, 'tp')
    vec_spec = P(None, 'tp')
    in_specs = (P('dp'), rep_spec, col_spec, col_spec, rep_spec, col_spec, col_spec, rep_spec, vec_spec, rep_spec, vec_spec, vec_spec, vec_spec, vec_spec, P(None, 'tp', None))

    def device_forward(hidden, norm_w, w_z, w_x, w_bc, w_dt, conv_x, conv_bc, bias_x, bias_bc, dt_bias, a_log, d_skip, gate_w, w_out):
        inner_width = w_x.shape[-1] * tp_size
        current = hidden
        for layer_idx in range(norm_w.shape[0]):
            current = mixer_layer(current, norm_w[layer_idx], w_z[layer_idx], w_x[layer_idx], w_bc[layer_idx], w_dt[layer_idx], conv_x[layer_idx], conv_bc[layer_idx], bias_x[layer_idx], bias_bc[layer_idx], dt_bias[layer_idx], a_log[layer_idx], d_skip[layer_idx], gate_w[layer_idx], w_out[layer_idx], inner_width)
        return current

    return jax.shard_map(device_forward, mesh=mesh, in_specs=in_specs, out_specs=P('dp'), check_vma=False)
```

profile of v0, /device:TPU:0, one launch (start us, length us, event | category | flops | bytes accessed | tf_op | source)
XLA Modules:
  0.0 1428.7 jit_solution(11270132750440298772)
XLA Ops:
  6.6 7.1 fusion
  13.9 7.9 fusion.21
  21.9 3.4 negate_multiply_fusion.1
  25.2 1.3 copy-done.1
  26.7 3.4 reduce-window.14
  30.7 0.2 broadcast.243
  31.1 0.5 slice_convert_fusion.4
  31.8 0.6 convert_reduce_fusion.7
  32.4 0.6 convert_reduce_fusion.2
  33.0 0.6 slice_convert_fusion.3
  33.6 0.6 convert_reduce_fusion.6
  34.7 0.2 copy.244
  35.2 8.3 convolution_convert_fusion.5
  43.5 2.9 divide_multiply_fusion.3
  46.5 1.6 fusion.118
  48.1 0.8 copy-done.31
  48.9 6.9 convolution_convert_fusion.3
  55.8 6.1 divide_multiply_fusion.1
  61.9 6.6 copy.190
  68.5 5.7 copy.248
  74.3 5.0 fusion.122
  79.3 3.8 broadcast_multiply_fusion.2
  83.1 10.8 fusion.45
  94.0 4.7 fusion.68
  98.7 30.5 %fusion.14 = f32[16,6,64,256]{3,2,1,0:T(8,128)S(1)} fusion(f32[16,256,256]{2,1,0:T(8,128)S(1)} %copy-done.7, f32[16,6,256]{2,1,0:T(8,128)S(1)} %copy.197, pred[256,256]{1,0:T(8,128)(4,1)S(1)} %iota_compare_fusion, f32[16,256,6,64]{1,0,3,2:T(8,128)S(1)} %bitcast.303), kind=kOutput, calls=%fused_computation.20 | convolution fusion | flops 4857004032 | bytes 16941056 | tf_op jit(solution)/shard_map/bchij,bcjhp->bcihp/dot_general | solution.py:37
  129.3 6.9 bitcast_add_fusion.1
  136.1 3.6 copy.210
  139.7 8.8 copy.251
  148.5 6.6 copy.211
  155.2 15.9 %multiply_reduce_fusion.1 = (f32[4096]{0:T(1024)S(1)}, f32[4096,384]{1,0:T(8,128)}) fusion(bf16[4096,1536]{1,0:T(8,128)(2,1)} %copy-done.1, bf16[2,1536,384]{2,1,0:T(8,128)(2,1)} %param.17, f32[4096,384]{1,0:T(8,128)} %copy.211, f32[1,4096,384]{2,1,0:T(8,128)} %divide_multiply_fusion.1, f32[384]{0:T(512)S(1)} %mul.533), kind=kOutput, calls=%fused_computation.70 | convolution fusion | flops 4849135616 | bytes 32654848 | tf_op jit(solution)/shard_map/btd,de->bte/dot_general | solution.py:59
  171.1 30.3 %psum.28 = f32[1,4096,1]{1,2,0:T(1,128)S(1)} all-reduce(f32[1,4096,1]{1,2,0:T(1,128)S(1)} %bitcast.324), channel_id=1, replica_groups=mesh['dp'=4,'tp'=8] {'tp'}, use_global_device_ids=true, to_apply=%region_5.6 | all-reduce | flops 4096 | bytes 32768 | tf_op jit(solution)/shard_map/psum | solution.py:71
  201.4 14.6 %convolution_bitcast_fusion.1 = f32[1,4096,1536]{2,1,0:T(8,128)} fusion(f32[4096,384]{1,0:T(8,128)} %get-tuple-element.58, f32[384]{0:T(512)S(1)} %get-tuple-element.16, f32[4096]{0:T(1024)S(1)} %bitcast.321, bf16[2,384,1536]{2,1,0:T(8,128)(2,1)S(1)} %copy-done.8), kind=kOutput, calls=%fused_computation.27 | convolution fusion | flops 4836556800 | bytes 32655360 | tf_op jit(solution)/shard_map/bte,ed->btd/dot_general | solution.py:73
  216.3 488.4 %all-reduce.7.cloned.1.call-done = f32[1,4096,1536]{2,1,0:T(8,128)} async-done(((f32[1,4096,1536]{2,1,0:T(8,128)}), f32[1,4096,1536]{2,1,0:T(8,128)}) %all-reduce.7.cloned.1.call-update) | async-done | bytes 25165840 | tf_op jit(solution)/shard_map/psum | solution.py:74
  704.7 13.2 fusion.4
  718.0 4.2 fusion.20
  722.2 0.2 copy-done
  722.4 3.4 negate_multiply_fusion
  725.8 1.4 copy-done.2
  727.4 3.4 reduce-window.16
  731.4 0.2 broadcast.248
  731.7 8.3 convolution_convert_fusion.4
  740.1 10.8 convolution_convert_fusion.1
  751.2 0.1 fusion.119
  751.4 0.2 copy.245
  751.9 3.3 divide_multiply_fusion.2
  755.3 1.6 fusion.117
  756.9 1.0 copy-done.5
  757.9 5.7 divide_multiply_fusion
  763.7 6.6 copy.213
  770.3 5.7 copy.252
  776.0 5.2 fusion.123
  781.2 3.8 broadcast_multiply_fusion
  785.1 10.8 fusion.42
  795.9 4.7 fusion.71
  800.6 30.5 %fusion.8 = f32[16,6,64,256]{3,2,1,0:T(8,128)S(1)} fusion(f32[16,256,256]{2,1,0:T(8,128)S(1)} %copy-done.6, f32[16,6,256]{2,1,0:T(8,128)S(1)} %copy.220, pred[256,256]{1,0:T(8,128)(4,1)S(1)} %iota_compare_fusion, f32[16,256,6,64]{1,0,3,2:T(8,128)S(1)} %bitcast.301), kind=kOutput, calls=%fused_computation.14 | convolution fusion | flops 4857004032 | bytes 16941056 | tf_op jit(solution)/shard_map/bchij,bcjhp->bcihp/dot_general | solution.py:37
  831.2 6.9 bitcast_add_fusion
  838.0 3.6 copy.233
  841.6 8.8 copy.255
  850.5 6.6 copy.234
  857.0 15.8 %multiply_reduce_fusion = (f32[4096]{0:T(1024)S(1)}, f32[4096,384]{1,0:T(8,128)}) fusion(bf16[4096,1536]{1,0:T(8,128)(2,1)} %copy-done.2, bf16[2,1536,384]{2,1,0:T(8,128)(2,1)} %param.17, f32[4096,384]{1,0:T(8,128)} %copy.234, f32[1,4096,384]{2,1,0:T(8,128)} %divide_multiply_fusion, f32[384]{0:T(512)S(1)} %mul.601), kind=kOutput, calls=%fused_computation.67 | convolution fusion | flops 4849135616 | bytes 32654848 | tf_op jit(solution)/shard_map/btd,de->bte/dot_general | solution.py:59
  872.9 28.1 %psum.30 = f32[1,4096,1]{1,2,0:T(1,128)S(1)} all-reduce(f32[1,4096,1]{1,2,0:T(1,128)S(1)} %bitcast.325), channel_id=1, replica_groups=mesh['dp'=4,'tp'=8] {'tp'}, use_global_device_ids=true, to_apply=%region_12.13 | all-reduce | flops 4096 | bytes 32768 | tf_op jit(solution)/shard_map/psum | solution.py:71
  901.1 14.7 %convolution_bitcast_fusion = f32[1,4096,1536]{2,1,0:T(8,128)} fusion(f32[4096,384]{1,0:T(8,128)} %get-tuple-element.62, f32[384]{0:T(512)S(1)} %copy-done.13, f32[4096]{0:T(1024)S(1)} %bitcast.320, bf16[2,384,1536]{2,1,0:T(8,128)(2,1)S(1)} %copy-done.9), kind=kOutput, calls=%fused_computation.26 | convolution fusion | flops 4836556800 | bytes 32655360 | tf_op jit(solution)/shard_map/bte,ed->btd/dot_general | solution.py:73
  915.7 488.5 %all-reduce.9.cloned.1.call-done = f32[1,4096,1536]{2,1,0:T(8,128)} async-done(((f32[1,4096,1536]{2,1,0:T(8,128)}), f32[1,4096,1536]{2,1,0:T(8,128)}) %all-reduce.9.cloned.1.call-update) | async-done | bytes 25165840 | tf_op jit(solution)/shard_map/psum | solution.py:74
  1404.3 17.3 %fusion.7 = bf16[1,4096,1536]{2,1,0:T(8,128)(2,1)} fusion(f32[1,4096,1536]{2,1,0:T(8,128)} %all-reduce.9.cloned.1.call-done, bf16[1,4096,1536]{2,1,0:T(8,128)(2,1)} %copy-done), kind=kLoop, calls=%fused_computation.13 | loop fusion | flops 18874368 | bytes 50331648 | tf_op jit(solution)/shard_map/convert_element_type | solution.py:75
  (143 shorter events, 3.8 us)
Async XLA Ops:
  6.5 698.2 %all-reduce.7.cloned.1.call-start = ((), (), s32[]{:S(2)}) async-start(), calls=%async_computation | async-start | bytes 50331648 | tf_op jit(solution)/shard_map/psum | solution.py:74
  6.6 7.2 copy-start.11
  6.6 7.2 copy-start.10
  6.6 7.3 copy-start.29
  6.6 7.3 copy-start.30
  21.8 4.8 copy-start.1
  21.8 9.3 copy-start.28
  21.8 9.3 copy-start.27
  21.8 10.0 copy-start.20
  21.8 10.6 copy-start.21
  21.8 11.2 copy-start.14
  21.8 11.7 copy-start.12
  35.2 12.9 slice-start
  35.2 12.9 slice-start.1
  43.5 4.6 slice-start.2
  46.5 2.4 copy-start.31
  68.5 5.8 copy-start.4
  83.1 15.5 %slice-start.5 = ((s8[6291456]{0:T(1024)(128)(4,1)}), s8[4194304]{0:T(1024)(128)(4,1)S(1)}, s32[]{:S(2)}) async-start(s8[6291456]{0:T(1024)(128)(4,1)} %bitcast.302), calls=%async_computation.7 | async-start | bytes 8388608
  83.1 15.5 %slice-start.6 = ((s8[6291456]{0:T(1024)(128)(4,1)}), s8[2097152]{0:T(1024)(128)(4,1)S(1)}, s32[]{:S(2)}) async-start(s8[6291456]{0:T(1024)(128)(4,1)} %bitcast.302), calls=%async_computation.8 | async-start | bytes 4194304
  83.1 15.6 %copy-start.7 = (f32[16,256,256]{2,1,0:T(8,128)S(1)}, f32[16,256,256]{2,1,0:T(8,128)}, u32[]{:S(2)}) copy-start(f32[16,256,256]{2,1,0:T(8,128)} %fusion.122) | copy-start | bytes 12582916
  155.2 46.3 %copy-start.8 = (bf16[2,384,1536]{2,1,0:T(8,128)(2,1)S(1)}, bf16[2,384,1536]{2,1,0:T(8,128)(2,1)}, u32[]{:S(2)}) copy-start(bf16[2,384,1536]{2,1,0:T(8,128)(2,1)} %param.29) | copy-start | bytes 7077892
  216.1 1188.2 %all-reduce.9.cloned.1.call-start = ((), (), s32[]{:S(2)}) async-start(), calls=%async_computation.1 | async-start | bytes 50331648 | tf_op jit(solution)/shard_map/psum | solution.py:74
  717.9 4.5 copy-start
  722.4 4.8 copy-start.2
  731.7 8.3 copy-start.32
  740.0 11.9 copy-start.22
  740.1 11.8 copy-start.23
  740.1 11.8 copy-start.24
  740.1 11.8 copy-start.25
  740.1 11.8 copy-start.26
  755.2 2.6 copy-start.5
  755.3 2.6 copy-start.15
  755.3 2.6 copy-start.16
  755.3 2.6 copy-start.17
  755.3 2.6 copy-start.18
  755.3 2.6 copy-start.19
  770.3 5.8 copy-start.3
  785.0 15.5 %slice-start.3 = ((s8[6291456]{0:T(1024)(128)(4,1)}), s8[4194304]{0:T(1024)(128)(4,1)S(1)}, s32[]{:S(2)}) async-start(s8[6291456]{0:T(1024)(128)(4,1)} %bitcast.300), calls=%async_computation.5 | async-start | bytes 8388608
  785.0 15.5 %slice-start.4 = ((s8[6291456]{0:T(1024)(128)(4,1)}), s8[2097152]{0:T(1024)(128)(4,1)S(1)}, s32[]{:S(2)}) async-start(s8[6291456]{0:T(1024)(128)(4,1)} %bitcast.300), calls=%async_computation.6 | async-start | bytes 4194304
  785.0 15.6 %copy-start.6 = (f32[16,256,256]{2,1,0:T(8,128)S(1)}, f32[16,256,256]{2,1,0:T(8,128)}, u32[]{:S(2)}) copy-start(f32[16,256,256]{2,1,0:T(8,128)} %fusion.123) | copy-start | bytes 12582916
  857.0 44.0 %copy-start.9 = (bf16[2,384,1536]{2,1,0:T(8,128)(2,1)S(1)}, bf16[2,384,1536]{2,1,0:T(8,128)(2,1)}, u32[]{:S(2)}) copy-start(bf16[2,384,1536]{2,1,0:T(8,128)(2,1)} %param.29) | copy-start | bytes 7077892
  857.0 44.0 %copy-start.13 = (f32[384]{0:T(512)S(1)}, f32[384]{0:T(512)}, u32[]{:S(2)}) copy-start(f32[384]{0:T(512)} %get-tuple-element.15) | copy-start | bytes 4612
Sparse Core Ops, SparseCore 0:
  216.2 488.4 all-reduce.6
  915.9 488.3 all-reduce.8
where the time goes:
time: 1430 us
  waiting for transfers between devices  977 us (68%)
  matrix products  218 us (15%)
  other arithmetic  85.9 us (6%)
  local copies, waits for them, and re-layouts  74.6 us (5%)
  blocking collectives  58.4 us (4%)
  between operations  14.6 us (1%)
    psum x2, waiting for transfers between devices, mixer_layer(): full_out = lax.psum(part_out, 'tp')  977 us
    dot_general x2, matrix products, ssd_blocks(): jnp.einsum('bchij,bcjhp->bcihp', mix_mat, x_dt, precision=FULL_PRECISION)  61.1 us
    psum x2, blocking collectives, mixer_layer(): total_sq = lax.psum(part_sq, 'tp')  58.4 us
    unnamed x88, local copies, waits for them, and re-layouts  34.1 us
    dot_general x2, matrix products, mixer_layer(): jnp.einsum('btd,de->bte', normed, w_z, preferred_element_type=jnp.float32)  31.7 us
    dot_general x2, matrix products, mixer_layer(): jnp.einsum('bte,ed->btd', normed_y, w_out, preferred_element_type=jnp.flo...  29.3 us
  transfers between devices with their start and end apart: 2, of which 2 were waited for; matrix products, arithmetic and copies ran while one was open for 0% of the time, Pallas kernels for 0%

commit v1 on v0

v1 whole, which is shorter than its diff:
```python
import functools

import jax
import jax.numpy as jnp
from jax import lax
from jax.experimental import pallas as pl
from jax.experimental.pallas import tpu as pltpu
from jax.sharding import PartitionSpec as P

EPSILON = 1e-5
CHUNK = 128
PAIR = 128
HEAD_DIM = 64
HIGHEST = lax.Precision.HIGHEST
F32 = jnp.float32
BF16 = jnp.bfloat16

LAG_B, LAG_H, LAG_M, LAG_O, LAG_T, LAG_F1, LAG_F2 = 3, 4, 6, 8, 10, 12, 13
N_V, N_STAT, N_PAIR, N_HOP, N_TOT = 4, 8, 4, 8, 16


def fdot(a, b):
    return jnp.dot(a, b, precision=HIGHEST, preferred_element_type=F32)


def bdot(a, b):
    return jnp.dot(a, b, preferred_element_type=F32)


def kernel(n_chunks, n_layers, tp, inner_width,
           hid, wz, wx, wbc, wdt, wo, par, out,
           cur, wzv, wxv, wbcv, wdtv, wov, conv_in, state, vbuf, stat,
           obuf, pairbuf, hbuf, rbuf_a, rbuf_b, tbuf, halfbuf,
           hid_sem, w_sem, out_sem,
           stat_send, stat_recv, pair_send, pair_recv, hop_send, hop_recv_a, hop_recv_b,
           tot_send_l, tot_send_r, tot_recv, half_send, half_recv):
    n_items = n_chunks * n_layers
    half = out.shape[1] // 2
    width = wz.shape[-1]
    n_pairs = width // PAIR
    me = lax.axis_index('tp')
    z = me // 2
    core = me % 2
    partner = z * 2 + (1 - core)

    def remote(src, dst, send, recv, device):
        return pltpu.make_async_remote_copy(src_ref=src, dst_ref=dst, send_sem=send, recv_sem=recv, device_id={'tp': device}, device_id_type=pl.DeviceIdType.MESH)

    def on_chip(k):
        return jnp.int32(k * 2) + core

    def chunk_rows(c):
        return pl.ds(pl.multiple_of(c * CHUNK, CHUNK), CHUNK)

    def hid_copy(c, k):
        return pltpu.make_async_copy(hid.at[chunk_rows(c), pl.ds(k * half, half)], cur.at[k, chunk_rows(c), :], hid_sem.at[c, k])

    def w_copies(l):
        return [
            pltpu.make_async_copy(wz.at[l], wzv.at[l], w_sem.at[l, 0]),
            pltpu.make_async_copy(wx.at[l], wxv.at[l], w_sem.at[l, 1]),
            pltpu.make_async_copy(wbc.at[l], wbcv.at[l], w_sem.at[l, 2]),
            pltpu.make_async_copy(wdt.at[l], wdtv.at[l], w_sem.at[l, 3]),
            pltpu.make_async_copy(wo.at[l, :, pl.ds(0, half)], wov.at[l, 0], w_sem.at[l, 4]),
            pltpu.make_async_copy(wo.at[l, :, pl.ds(half, half)], wov.at[l, 1], w_sem.at[l, 5]),
        ]

    def out_copy(c, k):
        return pltpu.make_async_copy(cur.at[k, chunk_rows(c), :], out.at[chunk_rows(c), pl.ds(k * half, half)], out_sem.at[c, k])

    for k in range(2):
        hid_copy(0, k).start()
    for copy in w_copies(0):
        copy.start()

    def start_hid(c, carry):
        for k in range(2):
            hid_copy(c, k).start()
        return carry

    lax.fori_loop(1, n_chunks, start_hid, 0)
    for l in range(1, n_layers):
        for copy in w_copies(l):
            copy.start()

    barrier = pltpu.get_barrier_semaphore()
    for d in range(1, tp):
        pl.semaphore_signal(barrier, inc=1, device_id={'tp': (me + d) % tp}, device_id_type=pl.DeviceIdType.MESH)
    pl.semaphore_wait(barrier, tp - 1)

    row_id = lax.broadcasted_iota(jnp.int32, (CHUNK, CHUNK), 0)
    col_id = lax.broadcasted_iota(jnp.int32, (CHUNK, CHUNK), 1)

    def stat_copy(m, d):
        slot = m % N_STAT
        return remote(stat.at[slot, me], stat.at[slot, me], stat_send.at[slot, d], stat_recv.at[slot, me], (me + d) % tp)

    def stat_arrival(m, d):
        slot = m % N_STAT
        peer = (me + d) % tp
        return remote(stat.at[slot, peer], stat.at[slot, peer], stat_send.at[slot, d], stat_recv.at[slot, peer], peer)

    def pair_copy(m):
        slot = m % N_PAIR
        return remote(obuf.at[slot], pairbuf.at[slot], pair_send.at[slot], pair_recv.at[slot], partner)

    def hop_a(m, device):
        slot = m % N_HOP
        return remote(hbuf.at[slot], rbuf_a.at[slot], hop_send.at[slot], hop_recv_a.at[slot], device)

    def hop_b(m, device):
        slot = m % N_HOP
        return remote(hbuf.at[slot], rbuf_b.at[slot], hop_send.at[slot], hop_recv_b.at[slot], device)

    def tot_left(m, device):
        slot = m % N_TOT
        return remote(tbuf.at[slot], tbuf.at[slot], tot_send_l.at[slot], tot_recv.at[slot], device)

    def tot_right(m, device):
        slot = m % N_TOT
        return remote(tbuf.at[slot], tbuf.at[slot], tot_send_r.at[slot], tot_recv.at[slot], device)

    def half_copy(m):
        return remote(tbuf.at[m % N_TOT], halfbuf.at[m % N_PAIR], half_send.at[m % N_PAIR], half_recv.at[m % N_PAIR], partner)

    def stage_a(m):
        l = m // n_chunks
        c = m % n_chunks

        @pl.when(l == 0)
        def _():
            for k in range(2):
                hid_copy(c, k).wait()

        @pl.when(c == 0)
        def _():
            for copy in w_copies(l):
                copy.wait()
            conv_in[0:8, :] = jnp.zeros((8, conv_in.shape[1]), F32)
            state[...] = jnp.zeros_like(state)

        rows = chunk_rows(c)
        u = jnp.concatenate([cur[0, rows, :], cur[1, rows, :]], axis=1).astype(F32)
        scale = lax.rsqrt(jnp.mean(u * u, axis=-1, keepdims=True) + EPSILON)
        h = (u * scale * par[l, 0:1, :]).astype(BF16)
        gate_z = bdot(h, wzv[l]).astype(BF16).astype(F32)
        conv_in[8:8 + CHUNK, 0:width] = bdot(h, wxv[l]).astype(BF16).astype(F32)
        conv_in[8:8 + CHUNK, width:] = bdot(h, wbcv[l]).astype(BF16).astype(F32)
        dt_pre = bdot(h, wdtv[l]).astype(BF16).astype(F32)

        cw = conv_in.shape[1]
        conv = par[l, 5:6, 0:cw]
        for j in range(4):
            conv = conv + conv_in[5 + j:5 + j + CHUNK, :] * par[l, 1 + j:2 + j, 0:cw]
        act = conv * jax.nn.sigmoid(conv)
        conv_in[0:8, :] = conv_in[CHUNK:CHUNK + 8, :]
        n_state = (cw - width) // 2
        b_in = act[:, width:width + n_state]
        c_in = act[:, width + n_state:]

        pre = dt_pre + par[l, 6:7, 0:PAIR]
        dt = jnp.maximum(pre, 0.0) + jnp.log1p(jnp.exp(-jnp.abs(pre)))
        a = -dt * jnp.exp(par[l, 7:8, 0:PAIR])
        lower = row_id >= col_id
        a_cum = fdot(jnp.where(lower, 1.0, 0.0).astype(F32), a)
        a_cum_t = a_cum.T
        a_last = a_cum[CHUNK - 1:CHUNK, :]
        grow = jnp.exp(a_cum)
        tail = jnp.exp(a_last - a_cum)
        carry = jnp.exp(a_last)
        c_dot_b = lax.dot_general(c_in, b_in, (((1,), (1,)), ((), ())), precision=HIGHEST, preferred_element_type=F32)
        b_t = b_in.T
        first = lax.broadcasted_iota(jnp.int32, (1, PAIR), 1) < HEAD_DIM
        v_slot = m % N_V
        sq = jnp.zeros((CHUNK, PAIR), F32)
        for p in range(n_pairs):
            lanes = slice(p * PAIR, (p + 1) * PAIR)

            def spread(q):
                return jnp.where(first, q[:, 2 * p:2 * p + 1], q[:, 2 * p + 1:2 * p + 2])

            def mix(n):
                seg = a_cum[:, n:n + 1] - a_cum_t[n:n + 1, :]
                return jnp.where(lower, jnp.exp(jnp.minimum(seg, 0.0)), 0.0) * c_dot_b

            x = act[:, lanes]
            x_dt = x * spread(dt)
            y_in = jnp.where(first, fdot(mix(2 * p), x_dt), fdot(mix(2 * p + 1), x_dt))
            s_in = state[:, lanes]
            y_st = fdot(c_in, s_in) * spread(grow)
            state[:, lanes] = s_in * spread(carry) + fdot(b_t, x_dt * spread(tail))
            y = y_in + y_st + par[l, 8:9, lanes] * x
            zp = gate_z[:, lanes]
            v = y * (zp * jax.nn.sigmoid(zp))
            vbuf[v_slot, :, lanes] = v
            sq = sq + v * v
        part = jnp.broadcast_to(jnp.sum(sq, axis=-1, keepdims=True), (CHUNK, PAIR)).T
        stat[m % N_STAT, me] = part[0:8, :]
        for d in range(1, tp):
            stat_copy(m, d).start()

    def stage_b(m):
        l = m // n_chunks
        for d in range(1, tp):
            stat_copy(m, d).wait_send()
            stat_arrival(m, d).wait_recv()
        slot = m % N_STAT
        total = stat[slot, 0]
        for s in range(1, tp):
            total = total + stat[slot, s]
        total = jnp.broadcast_to(total[0:1, :], (PAIR, CHUNK)).T
        scale = lax.rsqrt(total / inner_width + EPSILON)
        parts = []
        for p in range(n_pairs):
            lanes = slice(p * PAIR, (p + 1) * PAIR)
            parts.append((vbuf[m % N_V, :, lanes] * scale * par[l, 9:10, lanes]).astype(BF16))
        g = jnp.concatenate(parts, axis=1)
        obuf[m % N_PAIR] = bdot(g, wov[l, 1 - core])
        pair_copy(m).start()
        hbuf[m % N_HOP] = bdot(g, wov[l, core])

    def stage_h(m):
        pair_copy(m).wait()
        slot = m % N_HOP
        hbuf[slot] = hbuf[slot] + pairbuf[m % N_PAIR]

        @pl.when(z == 0)
        def _():
            hop_a(m, on_chip(1)).start()

        @pl.when(z == 3)
        def _():
            hop_a(m, on_chip(2)).start()

    def stage_m(m):
        @pl.when(z == 2)
        def _():
            hop_a(m, on_chip(3)).wait_recv()
            slot = m % N_HOP
            hbuf[slot] = hbuf[slot] + rbuf_a[slot]
            hop_b(m, on_chip(1)).start()

    def stage_o(m):
        @pl.when(z == 1)
        def _():
            hop_a(m, on_chip(0)).wait_recv()
            hop_b(m, on_chip(2)).wait_recv()
            slot = m % N_HOP
            tbuf[m % N_TOT] = rbuf_a[slot] + hbuf[slot] + rbuf_b[slot]
            tot_left(m, on_chip(0)).start()
            tot_right(m, on_chip(2)).start()

    def stage_t(m):
        @pl.when(z == 0)
        def _():
            hop_a(m, on_chip(1)).wait_send()
            tot_left(m, on_chip(1)).wait_recv()

        @pl.when(z == 1)
        def _():
            tot_left(m, on_chip(0)).wait_send()
            tot_right(m, on_chip(2)).wait_send()

        @pl.when(z == 2)
        def _():
            hop_b(m, on_chip(1)).wait_send()
            tot_right(m, on_chip(1)).wait_recv()
            tot_right(m, on_chip(3)).start()

        @pl.when(z == 3)
        def _():
            hop_a(m, on_chip(2)).wait_send()

    def stage_f1(m):
        @pl.when(z == 2)
        def _():
            tot_right(m, on_chip(3)).wait_send()

        @pl.when(z == 3)
        def _():
            tot_right(m, on_chip(2)).wait_recv()

        half_copy(m).start()

    def stage_f2(m):
        l = m // n_chunks
        c = m % n_chunks
        half_copy(m).wait()
        rows = chunk_rows(c)
        cur[core, rows, :] = (cur[core, rows, :].astype(F32) + tbuf[m % N_TOT]).astype(BF16)
        cur[1 - core, rows, :] = (cur[1 - core, rows, :].astype(F32) + halfbuf[m % N_PAIR]).astype(BF16)

        @pl.when(l == n_layers - 1)
        def _():
            for k in range(2):
                out_copy(c, k).start()

    def step(i, carry):
        for lag, stage in ((LAG_F2, stage_f2), (LAG_F1, stage_f1), (LAG_T, stage_t), (LAG_O, stage_o), (LAG_M, stage_m), (LAG_H, stage_h), (LAG_B, stage_b), (0, stage_a)):
            item = i - lag

            @pl.when(jnp.logical_and(item >= 0, item < n_items))
            def _(item=item, stage=stage):
                stage(item)
        return carry

    lax.fori_loop(0, n_items + LAG_F2, step, 0)

    def end_out(c, carry):
        for k in range(2):
            out_copy(c, k).wait()
        return carry

    lax.fori_loop(0, n_chunks, end_out, 0)


def solution(mesh):
    tp = mesh.shape['tp']
    rep_spec = P()
    col_spec = P(None, None, 'tp')
    vec_spec = P(None, 'tp')
    in_specs = (P('dp'), rep_spec, col_spec, col_spec, rep_spec, col_spec, col_spec, rep_spec, vec_spec, rep_spec, vec_spec, vec_spec, vec_spec, vec_spec, P(None, 'tp', None))

    def device_forward(hidden, norm_w, w_z, w_x, w_bc, w_dt, conv_x, conv_bc, bias_x, bias_bc, dt_bias, a_log, d_skip, gate_w, w_out):
        n_layers, d_model, width = w_z.shape
        n_steps = hidden.shape[1]
        n_chunks = n_steps // CHUNK
        bc_width = w_bc.shape[-1]
        heads = dt_bias.shape[-1]
        half = d_model // 2

        def line(v):
            v = v.astype(F32)
            v = v if v.ndim == 3 else v[:, None, :]
            return jnp.pad(v, ((0, 0), (0, 0), (0, d_model - v.shape[-1])))

        par = jnp.concatenate([
            line(norm_w),
            line(jnp.concatenate([conv_x, conv_bc], axis=-1)),
            line(jnp.concatenate([bias_x, bias_bc], axis=-1)),
            line(dt_bias), line(a_log), line(jnp.repeat(d_skip, HEAD_DIM, axis=-1)), line(gate_w),
        ], axis=1)
        w_dt = jnp.pad(w_dt, ((0, 0), (0, 0), (0, PAIR - heads)))

        any_spec = pl.BlockSpec(memory_space=pl.ANY)
        dma = pltpu.SemaphoreType.DMA
        block = (CHUNK, half)
        out = pl.pallas_call(
            functools.partial(kernel, n_chunks, n_layers, tp, width * tp),
            out_shape=jax.ShapeDtypeStruct((n_steps, d_model), BF16),
            in_specs=[any_spec] * 6 + [pl.BlockSpec(memory_space=pltpu.VMEM)],
            out_specs=any_spec,
            scratch_shapes=[
                pltpu.VMEM((2, n_steps, half), BF16),
                pltpu.VMEM((n_layers, d_model, width), BF16),
                pltpu.VMEM((n_layers, d_model, width), BF16),
                pltpu.VMEM((n_layers, d_model, bc_width), BF16),
                pltpu.VMEM((n_layers, d_model, PAIR), BF16),
                pltpu.VMEM((n_layers, 2, width, half), BF16),
                pltpu.VMEM((CHUNK + 8, width + bc_width), F32),
                pltpu.VMEM((bc_width // 2, width), F32),
                pltpu.VMEM((N_V, CHUNK, width), F32),
                pltpu.VMEM((N_STAT, tp, 8, CHUNK), F32),
                pltpu.VMEM((N_PAIR,) + block, F32),
                pltpu.VMEM((N_PAIR,) + block, F32),
                pltpu.VMEM((N_HOP,) + block, F32),
                pltpu.VMEM((N_HOP,) + block, F32),
                pltpu.VMEM((N_HOP,) + block, F32),
                pltpu.VMEM((N_TOT,) + block, F32),
                pltpu.VMEM((N_PAIR,) + block, F32),
                dma((n_chunks, 2)), dma((n_layers, 6)), dma((n_chunks, 2)),
                dma((N_STAT, tp)), dma((N_STAT, tp)), dma((N_PAIR,)), dma((N_PAIR,)),
                dma((N_HOP,)), dma((N_HOP,)), dma((N_HOP,)),
                dma((N_TOT,)), dma((N_TOT,)), dma((N_TOT,)), dma((N_PAIR,)), dma((N_PAIR,)),
            ],
            compiler_params=pltpu.CompilerParams(collective_id=0, has_side_effects=True, vmem_limit_bytes=60 * 1024 * 1024),
        )(hidden.reshape(n_steps, d_model), w_z, w_x, w_bc, w_dt, w_out, par)
        return out.reshape(1, n_steps, d_model)

    return jax.shard_map(device_forward, mesh=mesh, in_specs=in_specs, out_specs=P('dp'), check_vma=False)
```

time: 1430 us -> 650 us (0.45)
  waiting for transfers between devices: 977 us -> 0 us
  Pallas kernels: 0 us -> 626 us
  matrix products: 218 us -> 0 us
  other arithmetic: 85.9 us -> 0.74 us
  blocking collectives: 58.4 us -> 0 us
  local copies, waits for them, and re-layouts: 74.6 us -> 19.1 us
  between operations: 14.6 us -> 0.02 us
    psum x2 -> x0, waiting for transfers between devices: 977 us -> none  [mixer_layer(): full_out = lax.psum(part_out, 'tp')]
    pallas_call x0 -> x1, Pallas kernels: none -> 626 us  [device_forward(): pl.pallas_call(functools.partial(kernel, n_chunks, n_layers, tp, width *...]
    dot_general x20 -> x0, matrix products: 218 us -> none  [the longest x2 61.1 us: ssd_blocks(): jnp.einsum('bchij,bcjhp->bcihp', mix_mat, x_dt, precision=FULL_PRECISION)]
    psum x2 -> x0, blocking collectives: 58.4 us -> none  [mixer_layer(): total_sq = lax.psum(part_sq, 'tp')]
    mul x12 -> x0, other arithmetic: 27.2 us -> none  [the longest x2 11.9 us: mixer_layer(): x_act = jax.nn.silu(causal_conv(x_pre, conv_x, bias_x))]
    unnamed x88 -> x2, local copies, waits for them, and re-layouts: 34.1 us -> 11.7 us
    reduce_sum x2 -> x0, other arithmetic: 20.3 us -> none  [mixer_layer(): jnp.mean(residual * residual, axis=-1, keepdims=True) + EPSILON]
    convert_element_type x5 -> x0, other arithmetic: 19.1 us -> none  [the longest x1 17.3 us: mixer_layer(): return (residual + full_out).astype(jnp.bfloat16)]
  transfers between devices with their start and end apart: 2 -> 0, of which waited for: 2 -> 0; matrix products, arithmetic and copies ran while one was open for 0% -> 0% of each run, Pallas kernels for 0% -> 0%
where the time goes in v1:
time: 650 us; the launch traced here: 646 us
  Pallas kernels  626 us (96%)
  local copies, waits for them, and re-layouts  19.1 us (3%)
    pallas_call x1, Pallas kernels, device_forward(): pl.pallas_call(functools.partial(kernel, n_chunks, n_layers, tp, width *...  626 us

profile of v1, /device:TPU:0, one launch (start us, length us, event | category | flops | bytes accessed | tf_op | source)
XLA Modules:
  0.0 645.8 jit_solution(1698660565662029794)
XLA Ops:
  0.0 0.7 copy.21
  0.7 0.7 copy.20
  1.4 0.7 copy.25
  2.1 0.7 broadcast_in_dim.24
  2.8 0.1 broadcast_in_dim_reshape.4
  2.9 0.7 reshape.37
  3.6 0.7 pad.40
  4.3 0.7 pad.41
  5.0 0.7 fusion.3
  5.7 1.4 concatenate.24.par
  7.1 1.2 copy.19
  8.3 1.0 pad.35.wdt
  9.3 626.0 %shard_map.145 = bf16[4096,1536]{1,0:T(8,128)(2,1)} custom-call(bf16[4096,1536]{1,0:T(8,128)(2,1)} %bitcast.12, bf16[2,1536,384]{2,1,0:T(8,128)(2,1)} %wz.1, bf16[2,1536,384]{2,1,0:T(8,128)(2,1)} %wx.1, bf16[2,1536,256]{2,1,0:T(8,128)(2,1)} %wbc.1, bf16[2,1536,128]{2,1,0:T(8,128)(2,1)} %pad.35.wdt, bf16[2,384,1536]{2,1,0:T(8,128)(2,1)} %wo.1, ...), custom_call_target="tpu_custom_call" | custom-call | tf_op jit(solution)/shard_map/pallas_call | solution.py:348
  635.3 10.5 %copy.27 = bf16[1,4096,1536]{2,1,0:T(8,128)(2,1)} copy(bf16[1,4096,1536]{2,1,0:T(8,128)(2,1)} %bitcast.11) | data formatting | bytes 25165824
  (2 shorter events, 0.0 us)

commit v2 on v1

v2 whole, which is shorter than its diff:
```python
import functools

import jax
import jax.numpy as jnp
from jax import lax
from jax.experimental import pallas as pl
from jax.experimental.pallas import tpu as pltpu
from jax.sharding import PartitionSpec as P

EPSILON = 1e-5
CHUNK = 128
PAIR = 128
HEAD_DIM = 64
HIGHEST = lax.Precision.HIGHEST
F32 = jnp.float32
BF16 = jnp.bfloat16

LAG_B, LAG_H, LAG_M, LAG_O, LAG_T, LAG_F1, LAG_F2 = 3, 4, 6, 8, 10, 12, 13
N_V, N_STAT, N_PAIR, N_HOP, N_TOT = 4, 8, 4, 8, 16
EARLY_TWO, EARLY_ONE = 2, 5
SUB = 4
SUB_ROWS = CHUNK // SUB
AHEAD = 4
VMEM_BYTES = 67043328
ROW_CONV, ROW_BIAS, ROW_NORM, ROW_GATE, ROW_SKIP, ROW_DT, ROW_A = 0, 4, 5, 6, 7, 8, 9


def fdot(a, b):
    return jnp.dot(a, b, precision=HIGHEST, preferred_element_type=F32)


def bdot(a, b):
    return jnp.dot(a, b, preferred_element_type=F32)


def kernel(n_chunks, n_layers, tp, inner_width,
           hid, wz, wx, wbc, wo, small_0, small_1, small_2, small_3, small_4, small_5, small_6, small_7, small_8, small_9, cur,
           wzv, wxv, wbcv, wdtv, dt_rows, wov, par, conv_in, state, vbuf, stat,
           obuf, pairbuf, hbuf, rbuf_a, rbuf_b, tbuf, halfbuf,
           norm_w, wdt, conv_x, conv_bc, bias_x, bias_bc, dt_bias, a_log, d_skip, gate_w,
           hid_sem, w_sem, small_sem,
           stat_send, stat_recv, pair_send, pair_recv, hop_send, hop_recv_a, hop_recv_b,
           tot_send_l, tot_send_r, tot_recv, half_send, half_recv):
    n_items = n_chunks * n_layers
    half = cur.shape[1] // 2
    width = wz.shape[-1]
    bc_width = wbc.shape[-1]
    heads = dt_bias.shape[-1]
    n_pairs = width // PAIR
    n_chips = tp // 2
    me = lax.axis_index('tp')
    z = me // 2
    core = me % 2
    partner = z * 2 + (1 - core)
    role = z + core * (n_chips - 1 - 2 * z)

    def on_line(k):
        return (k + core * (n_chips - 1 - 2 * k)) * 2 + core

    def remote(src, dst, send, recv, device):
        return pltpu.make_async_remote_copy(src_ref=src, dst_ref=dst, send_sem=send, recv_sem=recv, device_id={'tp': device}, device_id_type=pl.DeviceIdType.MESH)

    def chunk_rows(c):
        return pl.ds(pl.multiple_of(c * CHUNK, CHUNK), CHUNK)

    def hid_copy(c):
        return pltpu.make_async_copy(hid.at[chunk_rows(c), :], cur.at[chunk_rows(c), :], hid_sem.at[c])

    def w_copies(l):
        return [
            pltpu.make_async_copy(wz.at[l], wzv.at[l], w_sem.at[l, 0]),
            pltpu.make_async_copy(wx.at[l], wxv.at[l], w_sem.at[l, 1]),
            pltpu.make_async_copy(wbc.at[l], wbcv.at[l], w_sem.at[l, 2]),
            pltpu.make_async_copy(wo.at[l, :, pl.ds(0, half)], wov.at[l, 0], w_sem.at[l, 3]),
            pltpu.make_async_copy(wo.at[l, :, pl.ds(half, half)], wov.at[l, 1], w_sem.at[l, 4]),
        ]

    sources = (small_0, small_1, small_2, small_3, small_4, small_5, small_6, small_7, small_8, small_9)
    small = [pltpu.make_async_copy(src, dst, small_sem.at[k]) for k, (src, dst) in enumerate(zip(sources, (norm_w, wdt, conv_x, conv_bc, bias_x, bias_bc, dt_bias, a_log, d_skip, gate_w)))]
    for copy in small:
        copy.start()
    hid_copy(0).start()
    for copy in w_copies(0):
        copy.start()
    for c in range(1, AHEAD):
        hid_copy(c).start()

    barrier = pltpu.get_barrier_semaphore()
    for d in range(1, tp):
        pl.semaphore_signal(barrier, inc=1, device_id={'tp': (me + d) % tp}, device_id_type=pl.DeviceIdType.MESH)

    par[...] = jnp.zeros_like(par)
    dt_rows[...] = jnp.zeros_like(dt_rows)
    wdtv[...] = jnp.zeros_like(wdtv)
    for copy in small:
        copy.wait()
    for l in range(n_layers):
        par[l, ROW_CONV:ROW_CONV + 4, 0:width] = conv_x[l].astype(F32)
        par[l, ROW_CONV:ROW_CONV + 4, width:width + bc_width] = conv_bc[l].astype(F32)
        par[l, ROW_BIAS:ROW_BIAS + 1, 0:width] = bias_x[...].astype(F32)[l:l + 1]
        par[l, ROW_BIAS:ROW_BIAS + 1, width:width + bc_width] = bias_bc[...].astype(F32)[l:l + 1]
        par[l, ROW_NORM:ROW_NORM + 1, :] = norm_w[...].astype(F32)[l:l + 1]
        par[l, ROW_GATE:ROW_GATE + 1, 0:width] = gate_w[...].astype(F32)[l:l + 1]
        par[l, ROW_SKIP:ROW_SKIP + 1, 0:heads] = d_skip[l:l + 1, :]
        par[l, ROW_DT:ROW_DT + 1, 0:heads] = dt_bias[l:l + 1, :]
        par[l, ROW_A:ROW_A + 1, 0:heads] = a_log[l:l + 1, :]
        for n in range(heads):
            dt_rows[n:n + 1, :] = wdt[n].astype(F32)[l:l + 1]
        wdtv[l, 0:dt_rows.shape[0], :] = dt_rows[...].astype(BF16)
    pl.semaphore_wait(barrier, tp - 1)

    row_id = lax.broadcasted_iota(jnp.int32, (CHUNK, CHUNK), 0)
    col_id = lax.broadcasted_iota(jnp.int32, (CHUNK, CHUNK), 1)

    def stat_copy(m, d):
        slot = m % N_STAT
        return remote(stat.at[slot, me], stat.at[slot, me], stat_send.at[slot, d], stat_recv.at[slot, me], (me + d) % tp)

    def stat_arrival(m, d):
        slot = m % N_STAT
        peer = (me + d) % tp
        return remote(stat.at[slot, peer], stat.at[slot, peer], stat_send.at[slot, d], stat_recv.at[slot, peer], peer)

    def pair_copy(m):
        slot = m % N_PAIR
        return remote(obuf.at[slot], pairbuf.at[slot], pair_send.at[slot], pair_recv.at[slot], partner)

    def sub(s):
        return pl.ds(s * SUB_ROWS, SUB_ROWS)

    def hop_a(m, s, device):
        slot = m % N_HOP
        return remote(hbuf.at[slot, sub(s)], rbuf_a.at[slot, sub(s)], hop_send.at[slot, s], hop_recv_a.at[slot, s], device)

    def hop_b(m, s, device):
        slot = m % N_HOP
        return remote(hbuf.at[slot, sub(s)], rbuf_b.at[slot, sub(s)], hop_send.at[slot, s], hop_recv_b.at[slot, s], device)

    def tot_back(m, s, device):
        slot = m % N_TOT
        return remote(tbuf.at[slot, sub(s)], tbuf.at[slot, sub(s)], tot_send_l.at[slot, s], tot_recv.at[slot, s], device)

    def tot_on(m, s, device):
        slot = m % N_TOT
        return remote(tbuf.at[slot, sub(s)], tbuf.at[slot, sub(s)], tot_send_r.at[slot, s], tot_recv.at[slot, s], device)

    def half_copy(m, s):
        slot = m % N_PAIR
        return remote(tbuf.at[m % N_TOT, sub(s)], halfbuf.at[slot, sub(s)], half_send.at[slot, s], half_recv.at[slot, s], partner)

    def stage_a(m):
        l = m // n_chunks
        c = m % n_chunks

        @pl.when(l == 0)
        def _():
            hid_copy(c).wait()

        @pl.when(m + AHEAD < n_chunks)
        def _():
            hid_copy(m + AHEAD).start()

        for later in range(1, n_layers):
            @pl.when(m == later * AHEAD)
            def _(later=later):
                for copy in w_copies(later):
                    copy.start()

        @pl.when(c == 0)
        def _():
            for copy in w_copies(l):
                copy.wait()
            conv_in[0:8, :] = jnp.zeros((8, conv_in.shape[1]), F32)
            state[...] = jnp.zeros_like(state)

        rows = chunk_rows(c)
        u = cur[rows, :].astype(F32)
        scale = lax.rsqrt(jnp.mean(u * u, axis=-1, keepdims=True) + EPSILON)
        h = (u * scale * par[l, ROW_NORM:ROW_NORM + 1, :]).astype(BF16)
        gate_z = bdot(h, wzv[l]).astype(BF16).astype(F32)
        conv_in[8:8 + CHUNK, 0:width] = bdot(h, wxv[l]).astype(BF16).astype(F32)
        conv_in[8:8 + CHUNK, width:] = bdot(h, wbcv[l]).astype(BF16).astype(F32)
        dt_pre = lax.dot_general(h, wdtv[l], (((1,), (1,)), ((), ())), preferred_element_type=F32).astype(BF16).astype(F32)

        cw = conv_in.shape[1]
        conv = par[l, ROW_BIAS:ROW_BIAS + 1, 0:cw]
        for j in range(4):
            conv = conv + conv_in[5 + j:5 + j + CHUNK, :] * par[l, ROW_CONV + j:ROW_CONV + j + 1, 0:cw]
        act = conv * jax.nn.sigmoid(conv)
        conv_in[0:8, :] = conv_in[CHUNK:CHUNK + 8, :]
        n_state = (cw - width) // 2
        b_in = act[:, width:width + n_state]
        c_in = act[:, width + n_state:]

        pre = dt_pre + par[l, ROW_DT:ROW_DT + 1, 0:PAIR]
        dt = jnp.maximum(pre, 0.0) + jnp.log1p(jnp.exp(-jnp.abs(pre)))
        a = -dt * jnp.exp(par[l, ROW_A:ROW_A + 1, 0:PAIR])
        lower = row_id >= col_id
        a_cum = fdot(jnp.where(lower, 1.0, 0.0).astype(F32), a)
        a_cum_t = a_cum.T
        a_last = a_cum[CHUNK - 1:CHUNK, :]
        grow = jnp.exp(a_cum)
        tail = jnp.exp(a_last - a_cum)
        carry = jnp.exp(a_last)
        c_dot_b = lax.dot_general(c_in, b_in, (((1,), (1,)), ((), ())), precision=HIGHEST, preferred_element_type=F32)
        b_t = b_in.T
        first = lax.broadcasted_iota(jnp.int32, (1, PAIR), 1) < HEAD_DIM
        v_slot = m % N_V
        sq = jnp.zeros((CHUNK, PAIR), F32)
        skip = par[l, ROW_SKIP:ROW_SKIP + 1, 0:PAIR]
        for p in range(n_pairs):
            lanes = slice(p * PAIR, (p + 1) * PAIR)

            def spread(q):
                return jnp.where(first, q[:, 2 * p:2 * p + 1], q[:, 2 * p + 1:2 * p + 2])

            def mix(n):
                seg = a_cum[:, n:n + 1] - a_cum_t[n:n + 1, :]
                return jnp.where(lower, jnp.exp(jnp.minimum(seg, 0.0)), 0.0) * c_dot_b

            x = act[:, lanes]
            x_dt = x * spread(dt)
            y_in = jnp.where(first, fdot(mix(2 * p), x_dt), fdot(mix(2 * p + 1), x_dt))
            s_in = state[:, lanes]
            y_st = fdot(c_in, s_in) * spread(grow)
            state[:, lanes] = s_in * spread(carry) + fdot(b_t, x_dt * spread(tail))
            y = y_in + y_st + spread(skip) * x
            zp = gate_z[:, lanes]
            v = y * (zp * jax.nn.sigmoid(zp))
            vbuf[v_slot, :, lanes] = v
            sq = sq + v * v
        part = jnp.broadcast_to(jnp.sum(sq, axis=-1, keepdims=True), (CHUNK, PAIR)).T
        stat[m % N_STAT, me] = part[0:8, :]
        for d in range(1, tp):
            stat_copy(m, d).start()

    def stage_b(m):
        l = m // n_chunks
        for d in range(1, tp):
            stat_copy(m, d).wait_send()
            stat_arrival(m, d).wait_recv()
        slot = m % N_STAT
        total = stat[slot, 0]
        for s in range(1, tp):
            total = total + stat[slot, s]
        total = jnp.broadcast_to(total[0:1, :], (PAIR, CHUNK)).T
        scale = lax.rsqrt(total / inner_width + EPSILON)
        parts = []
        for p in range(n_pairs):
            lanes = slice(p * PAIR, (p + 1) * PAIR)
            parts.append((vbuf[m % N_V, :, lanes] * scale * par[l, ROW_GATE:ROW_GATE + 1, lanes]).astype(BF16))
        g = jnp.concatenate(parts, axis=1)
        obuf[m % N_PAIR] = bdot(g, wov[l, 1 - core])
        pair_copy(m).start()
        hbuf[m % N_HOP] = bdot(g, wov[l, core])

    def stage_h(m):
        pair_copy(m).wait()
        slot = m % N_HOP
        hbuf[slot] = hbuf[slot] + pairbuf[m % N_PAIR]

        @pl.when(role == 0)
        def _():
            for s in range(SUB):
                hop_a(m, s, on_line(1)).start()

        @pl.when(role == 3)
        def _():
            for s in range(SUB):
                hop_a(m, s, on_line(2)).start()

    def stage_m(m):
        @pl.when(role == 2)
        def _():
            slot = m % N_HOP
            for s in range(SUB):
                hop_a(m, s, on_line(3)).wait_recv()
                hbuf[slot, sub(s)] = hbuf[slot, sub(s)] + rbuf_a[slot, sub(s)]
                hop_b(m, s, on_line(1)).start()

    def stage_o(m):
        @pl.when(role == 1)
        def _():
            slot = m % N_HOP
            for s in range(SUB):
                hop_a(m, s, on_line(0)).wait_recv()
                hop_b(m, s, on_line(2)).wait_recv()
                tbuf[m % N_TOT, sub(s)] = rbuf_a[slot, sub(s)] + hbuf[slot, sub(s)] + rbuf_b[slot, sub(s)]
                tot_on(m, s, on_line(2)).start()
                tot_back(m, s, on_line(0)).start()

    def stage_t(m):
        @pl.when(role == 0)
        def _():
            for s in range(SUB):
                hop_a(m, s, on_line(1)).wait_send()
                tot_back(m, s, on_line(1)).wait_recv()

        @pl.when(role == 1)
        def _():
            for s in range(SUB):
                tot_back(m, s, on_line(0)).wait_send()
                tot_on(m, s, on_line(2)).wait_send()

        @pl.when(role == 2)
        def _():
            for s in range(SUB):
                hop_b(m, s, on_line(1)).wait_send()
                tot_on(m, s, on_line(1)).wait_recv()
                tot_on(m, s, on_line(3)).start()

        @pl.when(role == 3)
        def _():
            for s in range(SUB):
                hop_a(m, s, on_line(2)).wait_send()

    def stage_f1(m):
        for s in range(SUB):
            @pl.when(role == 3)
            def _(s=s):
                tot_on(m, s, on_line(2)).wait_recv()

            half_copy(m, s).start()

    def stage_f2(m):
        @pl.when(role == 2)
        def _():
            for s in range(SUB):
                tot_on(m, s, on_line(3)).wait_send()

        own = pl.ds(pl.multiple_of(core * half, PAIR), half)
        other = pl.ds(pl.multiple_of((1 - core) * half, PAIR), half)
        for s in range(SUB):
            half_copy(m, s).wait()
            rows = pl.ds(pl.multiple_of((m % n_chunks) * CHUNK + s * SUB_ROWS, SUB_ROWS), SUB_ROWS)
            cur[rows, own] = (cur[rows, own].astype(F32) + tbuf[m % N_TOT, sub(s)]).astype(BF16)
            cur[rows, other] = (cur[rows, other].astype(F32) + halfbuf[m % N_PAIR, sub(s)]).astype(BF16)

    def step(i, carry):
        for lag, stage in ((LAG_F2, stage_f2), (LAG_F1, stage_f1), (LAG_T, stage_t), (LAG_O, stage_o), (LAG_M, stage_m), (LAG_H, stage_h), (LAG_B, stage_b)):
            k = i - lag
            item = jnp.where(k >= EARLY_ONE, k, jnp.where(k >= EARLY_TWO - 1, k + 1, k + 2))
            steady = jnp.logical_and(k >= EARLY_ONE, k < n_items)
            one_early = jnp.logical_and(k + 1 >= EARLY_TWO, k + 1 < EARLY_ONE)
            two_early = jnp.logical_and(k + 2 >= 0, k + 2 < EARLY_TWO)

            @pl.when(jnp.logical_or(steady, jnp.logical_or(one_early, two_early)))
            def _(item=item, stage=stage):
                stage(item)

        @pl.when(i < n_items)
        def _():
            stage_a(i)
        return carry

    lax.fori_loop(0, n_items + LAG_F2, step, 0)


def write_out(cur, out, sem):
    n_parts = sem.shape[0]
    rows = cur.shape[0] // n_parts
    copies = [pltpu.make_async_copy(cur.at[pl.ds(k * rows, rows)], out.at[pl.ds(k * rows, rows)], sem.at[k]) for k in range(n_parts)]
    for copy in copies:
        copy.start()
    for copy in copies:
        copy.wait()


def solution(mesh):
    tp = mesh.shape['tp']
    rep_spec = P()
    col_spec = P(None, None, 'tp')
    vec_spec = P(None, 'tp')
    in_specs = (P('dp'), rep_spec, col_spec, col_spec, rep_spec, col_spec, col_spec, rep_spec, vec_spec, rep_spec, vec_spec, vec_spec, vec_spec, vec_spec, P(None, 'tp', None))

    def device_forward(hidden, norm_w, w_z, w_x, w_bc, w_dt, conv_x, conv_bc, bias_x, bias_bc, dt_bias, a_log, d_skip, gate_w, w_out):
        n_layers, d_model, width = w_z.shape
        n_steps = hidden.shape[1]
        n_chunks = n_steps // CHUNK
        bc_width = w_bc.shape[-1]
        half = d_model // 2
        small = (norm_w, jnp.transpose(w_dt, (2, 0, 1)), conv_x, conv_bc, bias_x, bias_bc, dt_bias, a_log, d_skip, gate_w)
        hbm_spec = pl.BlockSpec(memory_space=pltpu.HBM)
        vmem_spec = pl.BlockSpec(memory_space=pltpu.VMEM)
        dma = pltpu.SemaphoreType.DMA
        block = (CHUNK, half)
        out = pl.pallas_call(
            functools.partial(kernel, n_chunks, n_layers, tp, width * tp),
            out_shape=pltpu.VMEM((n_steps, d_model), BF16),
            in_specs=[hbm_spec] * (5 + len(small)),
            out_specs=vmem_spec,
            scratch_shapes=[
                pltpu.VMEM((n_layers, d_model, width), BF16),
                pltpu.VMEM((n_layers, d_model, width), BF16),
                pltpu.VMEM((n_layers, d_model, bc_width), BF16),
                pltpu.VMEM((n_layers, PAIR, d_model), BF16),
                pltpu.VMEM((16, d_model), F32),
                pltpu.VMEM((n_layers, 2, width, half), BF16),
                pltpu.VMEM((n_layers, 16, d_model), F32),
                pltpu.VMEM((CHUNK + 8, width + bc_width), F32),
                pltpu.VMEM((bc_width // 2, width), F32),
                pltpu.VMEM((N_V, CHUNK, width), F32),
                pltpu.VMEM((N_STAT, tp, 8, CHUNK), F32),
                pltpu.VMEM((N_PAIR,) + block, F32),
                pltpu.VMEM((N_PAIR,) + block, F32),
                pltpu.VMEM((N_HOP,) + block, F32),
                pltpu.VMEM((N_HOP,) + block, F32),
                pltpu.VMEM((N_HOP,) + block, F32),
                pltpu.VMEM((N_TOT,) + block, F32),
                pltpu.VMEM((N_PAIR,) + block, F32),
                *[pltpu.VMEM(v.shape, v.dtype) for v in small],
                dma((n_chunks,)), dma((n_layers, 5)), dma((len(small),)),
                dma((N_STAT, tp)), dma((N_STAT, tp)), dma((N_PAIR,)), dma((N_PAIR,)),
                dma((N_HOP, SUB)), dma((N_HOP, SUB)), dma((N_HOP, SUB)),
                dma((N_TOT, SUB)), dma((N_TOT, SUB)), dma((N_TOT, SUB)), dma((N_PAIR, SUB)), dma((N_PAIR, SUB)),
            ],
            compiler_params=pltpu.CompilerParams(collective_id=0, has_side_effects=True, vmem_limit_bytes=VMEM_BYTES - 2 * n_steps * d_model),
        )(hidden.reshape(n_steps, d_model), w_z, w_x, w_bc, w_out, *small)
        out = pl.pallas_call(
            write_out,
            out_shape=jax.ShapeDtypeStruct((n_steps, d_model), BF16),
            in_specs=[vmem_spec],
            out_specs=hbm_spec,
            scratch_shapes=[dma((8,))],
            compiler_params=pltpu.CompilerParams(vmem_limit_bytes=1024 * 1024),
        )(out)
        return out.reshape(1, n_steps, d_model)

    return jax.shard_map(device_forward, mesh=mesh, in_specs=in_specs, out_specs=P('dp'), check_vma=False)
```

time: 650 us -> 629 us (0.968)
  local copies, waits for them, and re-layouts: 19.1 us -> 0 us
    unnamed x2 -> x0, local copies, waits for them, and re-layouts: 11.7 us -> none
where the time goes in v2:
time: 629 us
  Pallas kernels  629 us (100%)
    pallas_call x1, Pallas kernels, device_forward(): pl.pallas_call(functools.partial(kernel, n_chunks, n_layers, tp, width *...  625 us

profile of v2, /device:TPU:0, one launch (start us, length us, event | category | flops | bytes accessed | tf_op | source)
XLA Modules:
  0.0 629.2 jit_solution(8502890213252531010)
XLA Ops:
  0.0 624.6 %shard_map.145.cur = bf16[4096,1536]{1,0:T(8,128)(2,1)S(1)} custom-call(bf16[4096,1536]{1,0:T(8,128)(2,1)} %bitcast.3, bf16[2,1536,384]{2,1,0:T(8,128)(2,1)} %wz.1, bf16[2,1536,384]{2,1,0:T(8,128)(2,1)} %wx.1, bf16[2,1536,256]{2,1,0:T(8,128)(2,1)} %wbc.1, bf16[2,384,1536]{2,1,0:T(8,128)(2,1)} %wo.1, bf16[2,1536]{1,0:T(2,128)(2,1)} %small_0.1, ...), custom_call_target="tpu_custom_call" | custom-call | tf_op jit(solution)/shard_map/pallas_call | solution.py:387
  624.6 4.7 shard_map.146

commit v3 on v2

--- a/solution.py
+++ b/solution.py
@@ -15,10 +15,10 @@
 F32 = jnp.float32
 BF16 = jnp.bfloat16
 
-LAG_B, LAG_H, LAG_M, LAG_O, LAG_T, LAG_F1, LAG_F2 = 3, 4, 6, 8, 10, 12, 13
+LAG_B, LAG_H, LAG_M, LAG_O, LAG_T, LAG_F1, LAG_F2 = 3, 3, 5, 7, 9, 11, 12
 N_V, N_STAT, N_PAIR, N_HOP, N_TOT = 4, 8, 4, 8, 16
 EARLY_TWO, EARLY_ONE = 2, 5
-SUB = 4
+SUB = 1
 SUB_ROWS = CHUNK // SUB
 AHEAD = 4
 VMEM_BYTES = 67043328
@@ -336,21 +336,26 @@
             cur[rows, own] = (cur[rows, own].astype(F32) + tbuf[m % N_TOT, sub(s)]).astype(BF16)
             cur[rows, other] = (cur[rows, other].astype(F32) + halfbuf[m % N_PAIR, sub(s)]).astype(BF16)
 
+    def later_stage(i, lag, stage):
+        k = i - lag
+        item = jnp.where(k >= EARLY_ONE, k, jnp.where(k >= EARLY_TWO - 1, k + 1, k + 2))
+        steady = jnp.logical_and(k >= EARLY_ONE, k < n_items)
+        one_early = jnp.logical_and(k + 1 >= EARLY_TWO, k + 1 < EARLY_ONE)
+        two_early = jnp.logical_and(k + 2 >= 0, k + 2 < EARLY_TWO)
+
+        @pl.when(jnp.logical_or(steady, jnp.logical_or(one_early, two_early)))
+        def _():
+            stage(item)
+
     def step(i, carry):
-        for lag, stage in ((LAG_F2, stage_f2), (LAG_F1, stage_f1), (LAG_T, stage_t), (LAG_O, stage_o), (LAG_M, stage_m), (LAG_H, stage_h), (LAG_B, stage_b)):
-            k = i - lag
-            item = jnp.where(k >= EARLY_ONE, k, jnp.where(k >= EARLY_TWO - 1, k + 1, k + 2))
-            steady = jnp.logical_and(k >= EARLY_ONE, k < n_items)
-            one_early = jnp.logical_and(k + 1 >= EARLY_TWO, k + 1 < EARLY_ONE)
-            two_early = jnp.logical_and(k + 2 >= 0, k + 2 < EARLY_TWO)
-
-            @pl.when(jnp.logical_or(steady, jnp.logical_or(one_early, two_early)))
-            def _(item=item, stage=stage):
-                stage(item)
+        for lag, stage in ((LAG_F2, stage_f2), (LAG_F1, stage_f1), (LAG_T, stage_t), (LAG_O, stage_o), (LAG_M, stage_m), (LAG_B, stage_b)):
+            later_stage(i, lag, stage)
 
         @pl.when(i < n_items)
         def _():
             stage_a(i)
+
+        later_stage(i, LAG_H, stage_h)
         return carry
 
     lax.fori_loop(0, n_items + LAG_F2, step, 0)

time: 629 us -> 633 us (level)
  no operation moved by 1% of the time
where the time goes in v3:
time: 633 us
  Pallas kernels  633 us (100%)
    pallas_call x1, Pallas kernels, device_forward(): pl.pallas_call(functools.partial(kernel, n_chunks, n_layers, tp, width *...  628 us

profile of v3, /device:TPU:0, one launch (start us, length us, event | category | flops | bytes accessed | tf_op | source)
XLA Modules:
  0.0 632.8 jit_solution(14785918948453902572)
XLA Ops:
  0.0 628.1 %shard_map.145.cur = bf16[4096,1536]{1,0:T(8,128)(2,1)S(1)} custom-call(bf16[4096,1536]{1,0:T(8,128)(2,1)} %bitcast.3, bf16[2,1536,384]{2,1,0:T(8,128)(2,1)} %wz.1, bf16[2,1536,384]{2,1,0:T(8,128)(2,1)} %wx.1, bf16[2,1536,256]{2,1,0:T(8,128)(2,1)} %wbc.1, bf16[2,384,1536]{2,1,0:T(8,128)(2,1)} %wo.1, bf16[2,1536]{1,0:T(2,128)(2,1)} %small_0.1, ...), custom_call_target="tpu_custom_call" | custom-call | tf_op jit(solution)/shard_map/pallas_call | solution.py:392
  628.1 4.7 shard_map.146

commit v4 on v2

--- a/solution.py
+++ b/solution.py
@@ -230,7 +230,7 @@
             vbuf[v_slot, :, lanes] = v
             sq = sq + v * v
         part = jnp.broadcast_to(jnp.sum(sq, axis=-1, keepdims=True), (CHUNK, PAIR)).T
-        stat[m % N_STAT, me] = part[0:8, :]
+        stat[m % N_STAT, me] = part[0:1, :]
         for d in range(1, tp):
             stat_copy(m, d).start()
 
@@ -243,7 +243,7 @@
         total = stat[slot, 0]
         for s in range(1, tp):
             total = total + stat[slot, s]
-        total = jnp.broadcast_to(total[0:1, :], (PAIR, CHUNK)).T
+        total = jnp.broadcast_to(total, (PAIR, CHUNK)).T
         scale = lax.rsqrt(total / inner_width + EPSILON)
         parts = []
         for p in range(n_pairs):
@@ -400,7 +400,7 @@
                 pltpu.VMEM((CHUNK + 8, width + bc_width), F32),
                 pltpu.VMEM((bc_width // 2, width), F32),
                 pltpu.VMEM((N_V, CHUNK, width), F32),
-                pltpu.VMEM((N_STAT, tp, 8, CHUNK), F32),
+                pltpu.VMEM((N_STAT, tp, 1, CHUNK), F32),
                 pltpu.VMEM((N_PAIR,) + block, F32),
                 pltpu.VMEM((N_PAIR,) + block, F32),
                 pltpu.VMEM((N_HOP,) + block, F32),

time: 629 us -> 604 us (0.960)
  Pallas kernels: 629 us -> 604 us
    pallas_call x1, Pallas kernels: 625 us -> 599 us  [device_forward(): pl.pallas_call(functools.partial(kernel, n_chunks, n_layers, tp, width *...]
where the time goes in v4:
time: 604 us
  Pallas kernels  604 us (100%)
    pallas_call x1, Pallas kernels, device_forward(): pl.pallas_call(functools.partial(kernel, n_chunks, n_layers, tp, width *...  599 us

profile of v4, /device:TPU:0, one launch (start us, length us, event | category | flops | bytes accessed | tf_op | source)
XLA Modules:
  0.0 603.9 jit_solution(13919712447194370161)
XLA Ops:
  0.0 599.2 %shard_map.145.cur = bf16[4096,1536]{1,0:T(8,128)(2,1)S(1)} custom-call(bf16[4096,1536]{1,0:T(8,128)(2,1)} %bitcast.3, bf16[2,1536,384]{2,1,0:T(8,128)(2,1)} %wz.1, bf16[2,1536,384]{2,1,0:T(8,128)(2,1)} %wx.1, bf16[2,1536,256]{2,1,0:T(8,128)(2,1)} %wbc.1, bf16[2,384,1536]{2,1,0:T(8,128)(2,1)} %wo.1, bf16[2,1536]{1,0:T(2,128)(2,1)} %small_0.1, ...), custom_call_target="tpu_custom_call" | custom-call | tf_op jit(solution)/shard_map/pallas_call | solution.py:387
  599.3 4.7 shard_map.146

commit v5 on v4

--- a/solution.py
+++ b/solution.py
@@ -15,7 +15,7 @@
 F32 = jnp.float32
 BF16 = jnp.bfloat16
 
-LAG_B, LAG_H, LAG_M, LAG_O, LAG_T, LAG_F1, LAG_F2 = 3, 4, 6, 8, 10, 12, 13
+LAG_B, LAG_H, LAG_M, LAG_O, LAG_T, LAG_F1, LAG_F2 = 3, 4, 6, 7, 8, 9, 10
 N_V, N_STAT, N_PAIR, N_HOP, N_TOT = 4, 8, 4, 8, 16
 EARLY_TWO, EARLY_ONE = 2, 5
 SUB = 4
@@ -107,7 +107,6 @@
         for n in range(heads):
             dt_rows[n:n + 1, :] = wdt[n].astype(F32)[l:l + 1]
         wdtv[l, 0:dt_rows.shape[0], :] = dt_rows[...].astype(BF16)
-    pl.semaphore_wait(barrier, tp - 1)
 
     row_id = lax.broadcasted_iota(jnp.int32, (CHUNK, CHUNK), 0)
     col_id = lax.broadcasted_iota(jnp.int32, (CHUNK, CHUNK), 1)
@@ -148,7 +147,7 @@
         slot = m % N_PAIR
         return remote(tbuf.at[m % N_TOT, sub(s)], halfbuf.at[slot, sub(s)], half_send.at[slot, s], half_recv.at[slot, s], partner)
 
-    def stage_a(m):
+    def stage_a(m, before_send=None):
         l = m // n_chunks
         c = m % n_chunks
 
@@ -231,6 +230,8 @@
             sq = sq + v * v
         part = jnp.broadcast_to(jnp.sum(sq, axis=-1, keepdims=True), (CHUNK, PAIR)).T
         stat[m % N_STAT, me] = part[0:1, :]
+        if before_send is not None:
+            before_send()
         for d in range(1, tp):
             stat_copy(m, d).start()
 
@@ -353,7 +354,8 @@
             stage_a(i)
         return carry
 
-    lax.fori_loop(0, n_items + LAG_F2, step, 0)
+    stage_a(jnp.int32(0), lambda: pl.semaphore_wait(barrier, tp - 1))
+    lax.fori_loop(1, n_items + LAG_F2, step, 0)
 
 
 def write_out(cur, out, sem):

time: 604 us -> 609 us (level)
  no operation moved by 1% of the time
where the time goes in v5:
time: 609 us; the launch traced here: 605 us
  Pallas kernels  605 us (99%)
    pallas_call x1, Pallas kernels, device_forward(): pl.pallas_call(functools.partial(kernel, n_chunks, n_layers, tp, width *...  600 us

profile of v5, /device:TPU:0, one launch (start us, length us, event | category | flops | bytes accessed | tf_op | source)
XLA Modules:
  0.0 605.1 jit_solution(7392167442067308451)
XLA Ops:
  0.0 600.4 %shard_map.145.cur = bf16[4096,1536]{1,0:T(8,128)(2,1)S(1)} custom-call(bf16[4096,1536]{1,0:T(8,128)(2,1)} %bitcast.3, bf16[2,1536,384]{2,1,0:T(8,128)(2,1)} %wz.1, bf16[2,1536,384]{2,1,0:T(8,128)(2,1)} %wx.1, bf16[2,1536,256]{2,1,0:T(8,128)(2,1)} %wbc.1, bf16[2,384,1536]{2,1,0:T(8,128)(2,1)} %wo.1, bf16[2,1536]{1,0:T(2,128)(2,1)} %small_0.1, ...), custom_call_target="tpu_custom_call" | custom-call | tf_op jit(solution)/shard_map/pallas_call | solution.py:389
  600.4 4.7 shard_map.146

commit v6 on v5

--- a/solution.py
+++ b/solution.py
@@ -15,7 +15,7 @@
 F32 = jnp.float32
 BF16 = jnp.bfloat16
 
-LAG_B, LAG_H, LAG_M, LAG_O, LAG_T, LAG_F1, LAG_F2 = 3, 4, 6, 7, 8, 9, 10
+LAG_B, LAG_H, LAG_M, LAG_O, LAG_T, LAG_F1, LAG_F2 = 3, 4, 6, 7, 9, 11, 12
 N_V, N_STAT, N_PAIR, N_HOP, N_TOT = 4, 8, 4, 8, 16
 EARLY_TWO, EARLY_ONE = 2, 5
 SUB = 4
@@ -201,11 +201,14 @@
         grow = jnp.exp(a_cum)
         tail = jnp.exp(a_last - a_cum)
         carry = jnp.exp(a_last)
-        c_dot_b = lax.dot_general(c_in, b_in, (((1,), (1,)), ((), ())), precision=HIGHEST, preferred_element_type=F32)
         b_t = b_in.T
+        s_in = state[...]
+        from_c = fdot(c_in, jnp.concatenate([b_t, s_in], axis=1))
+        c_dot_b = from_c[:, 0:CHUNK]
         first = lax.broadcasted_iota(jnp.int32, (1, PAIR), 1) < HEAD_DIM
         v_slot = m % N_V
         sq = jnp.zeros((CHUNK, PAIR), F32)
+        x_tail, carries = [], []
         skip = par[l, ROW_SKIP:ROW_SKIP + 1, 0:PAIR]
         for p in range(n_pairs):
             lanes = slice(p * PAIR, (p + 1) * PAIR)
@@ -219,15 +222,18 @@
 
             x = act[:, lanes]
             x_dt = x * spread(dt)
-            y_in = jnp.where(first, fdot(mix(2 * p), x_dt), fdot(mix(2 * p + 1), x_dt))
-            s_in = state[:, lanes]
-            y_st = fdot(c_in, s_in) * spread(grow)
-            state[:, lanes] = s_in * spread(carry) + fdot(b_t, x_dt * spread(tail))
+            mixes = jnp.concatenate([mix(2 * p), mix(2 * p + 1)], axis=1)
+            x_both = jnp.concatenate([jnp.where(first, x_dt, 0.0), jnp.where(first, 0.0, x_dt)], axis=0)
+            y_in = fdot(mixes, x_both)
+            y_st = from_c[:, CHUNK + p * PAIR:CHUNK + (p + 1) * PAIR] * spread(grow)
+            x_tail.append(x_dt * spread(tail))
+            carries.append(spread(carry))
             y = y_in + y_st + spread(skip) * x
             zp = gate_z[:, lanes]
             v = y * (zp * jax.nn.sigmoid(zp))
             vbuf[v_slot, :, lanes] = v
             sq = sq + v * v
+        state[...] = s_in * jnp.concatenate(carries, axis=1) + fdot(b_t, jnp.concatenate(x_tail, axis=1))
         part = jnp.broadcast_to(jnp.sum(sq, axis=-1, keepdims=True), (CHUNK, PAIR)).T
         stat[m % N_STAT, me] = part[0:1, :]
         if before_send is not None:

time: 609 us -> 598 us (0.982)
  Pallas kernels: 605 us -> 598 us
    pallas_call x1, Pallas kernels: 600 us -> 593 us  [device_forward(): pl.pallas_call(functools.partial(kernel, n_chunks, n_layers, tp, width *...]
where the time goes in v6:
time: 598 us
  Pallas kernels  598 us (100%)
    pallas_call x1, Pallas kernels, device_forward(): pl.pallas_call(functools.partial(kernel, n_chunks, n_layers, tp, width *...  593 us

profile of v6, /device:TPU:0, one launch (start us, length us, event | category | flops | bytes accessed | tf_op | source)
XLA Modules:
  0.0 598.1 jit_solution(608721476053243498)
XLA Ops:
  0.0 593.5 %shard_map.145.cur = bf16[4096,1536]{1,0:T(8,128)(2,1)S(1)} custom-call(bf16[4096,1536]{1,0:T(8,128)(2,1)} %bitcast.3, bf16[2,1536,384]{2,1,0:T(8,128)(2,1)} %wz.1, bf16[2,1536,384]{2,1,0:T(8,128)(2,1)} %wx.1, bf16[2,1536,256]{2,1,0:T(8,128)(2,1)} %wbc.1, bf16[2,384,1536]{2,1,0:T(8,128)(2,1)} %wo.1, bf16[2,1536]{1,0:T(2,128)(2,1)} %small_0.1, ...), custom_call_target="tpu_custom_call" | custom-call | tf_op jit(solution)/shard_map/pallas_call | solution.py:395
  593.5 4.7 shard_map.146
